TPU v7x, 32 devices: a whole 2x2x4 slice. The times are simulated.
32 devices in a mesh: grp: 2 (over y), row: 4 (over x, core), col: 4 (over z).
Axes of the slice: x: 2, y: 2, z: 4, core: 2. Of those that a mesh axis runs over, the one named last changes fastest.
Arguments:
- perturbation: bfloat16 [4, 12000, 12000], P('grp', 'row', 'col'), parts along dimension 0, may hold values from -96 to 96
- occ_coeffs: bfloat16 [12000, 2000], P('row', 'col'), may hold values from -0.0546875 to 0.0546875
- vir_coeffs: bfloat16 [12000, 512], P('col', 'row'), may hold values from -0.0546875 to 0.0546875
- occ_energies: float32 [2000], replicated, may hold values from -1 to -0.1
- vir_energies: float32 [512], replicated, may hold values from 0.1 to 1.5
Outputs:
- density_response: bfloat16 [4, 12000, 12000], P('grp', 'row', 'col'), parts along dimension 0
There are 2 independent parts, one for each index of `grp`. A program takes and returns all parts, laid end to end along the dimension named above; an argument that names none is the same for every part. Nothing has to cross between parts.
All inputs are finite; a program needn't handle non-finite values.
Results may differ from a plain program's by a relative error of at most 0.0098.
Values may be sent and summed in bfloat16 or wider, within the bound.
A program may use at most 192 MiB of HBM per device.

v0:
```python
import jax
import jax.numpy as jnp
from jax import lax
from jax.sharding import PartitionSpec as P

BF16 = jnp.bfloat16
F32 = jnp.float32


def per_device(perturbation, occ_coeffs, vir_coeffs, occ_energies, vir_energies):
    vir_rows = lax.all_gather(vir_coeffs, "row", axis=1, tiled=True)
    occ_parts = lax.all_gather(occ_coeffs, "col")
    cols, _, width = occ_parts.shape
    image = jnp.einsum("pij,jv->piv", perturbation, vir_rows, preferred_element_type=F32).astype(
        BF16
    )
    part = jnp.einsum("cio,piv->pcov", occ_parts, image, preferred_element_type=F32).astype(BF16)
    coupling = lax.psum(part, ("row", "col"))
    gaps = occ_energies.reshape(cols, width)[:, :, None] - vir_energies[None, None, :]
    response = (coupling.astype(F32) / gaps[None]).astype(BF16)
    mixed = jnp.einsum("cio,pcov->piv", occ_parts, response, preferred_element_type=F32).astype(
        BF16
    )
    return jnp.einsum("piv,jv->pij", mixed, vir_rows, preferred_element_type=F32).astype(BF16)


def solution(mesh):
    placed = (P("grp", "row", "col"), P("row", "col"), P("col", "row"), P(), P())
    return jax.shard_map(
        per_device, mesh=mesh, in_specs=placed, out_specs=P("grp", "row", "col"), check_vma=False
    )
```

profile of v0, /device:TPU:0, one launch (start us, length us, event | category | flops | bytes accessed | tf_op | source)
XLA Modules:
  0.0 448.0 jit_solution(10581064769501468559)
XLA Ops:
  6.5 0.0 all-gather.4.cloned.1.call-start
  6.5 0.7 all-gather.4.cloned.1.call-update
  7.3 0.0 all-gather.6.cloned.1.call-start
  7.3 0.7 all-gather.6.cloned.1.call-update
  8.0 0.0 all-reduce.2.cloned.1.call-start
  8.1 32.1 %all-gather.4.cloned.1.call-done = bf16[3000,512]{1,0:T(8,128)(2,1)} async-done(((bf16[3000,128]{1,0:T(8,128)(2,1)}), bf16[3000,512]{1,0:T(8,128)(2,1)}) %all-gather.4.cloned.1.call-update) | async-done | bytes 3072016 | tf_op jit(solution)/shard_map/all_gather | solution.py:11
  40.1 25.8 %fusion.45 = bf16[2,3000,512,1]{2,1,3,0:T(8,128)(2,1)} fusion(bf16[2,3000,3000]{2,1,0:T(8,128)(2,1)} %param.5, bf16[3000,512]{1,0:T(8,128)(2,1)} %all-gather.4.cloned.1.call-done), kind=kOutput, calls=%fused_computation.5.clone.clone.clone.1 | convolution fusion | flops 18435072000 | bytes 45216000 | tf_op jit(solution)/shard_map/pij,jv->piv/dot_general | solution.py:14
  66.0 189.1 %all-gather.6.cloned.1.call-done = bf16[12000,500]{1,0:T(8,128)(2,1)} async-done(((bf16[3000,500]{1,0:T(8,128)(2,1)}), bf16[12000,500]{1,0:T(8,128)(2,1)}) %all-gather.6.cloned.1.call-update) | async-done | bytes 12000016 | tf_op jit(solution)/shard_map/all_gather | solution.py:12
  255.1 19.1 %fusion.17 = bf16[2,512,4,500]{1,3,2,0:T(8,128)(2,1)} fusion(bf16[4,3000,500,1]{2,1,0,3:T(8,128)(2,1)} %bitcast.58, bf16[2,3000,512,1]{2,1,3,0:T(8,128)(2,1)} %fusion.45), kind=kOutput, calls=%fused_computation.12 | convolution fusion | flops 12290048000 | bytes 22240000 | tf_op jit(solution)/shard_map/cio,piv->pcov/dot_general | solution.py:17
  274.2 0.0 copy-start
  274.2 0.0 copy-start.1
  274.2 7.8 %copy.10 = bf16[2,512,4,500]{3,2,1,0:T(4,128)(2,1)} copy(bf16[2,512,4,500]{1,3,2,0:T(8,128)(2,1)} %fusion.17) | data formatting | bytes 8192000
  282.0 0.0 all-reduce.2.cloned.1.call-update
  282.0 0.0 copy-done
  282.1 0.1 sub.19
  282.1 0.0 copy-done.1
  282.1 2.8 broadcast_subtract_fusion
  285.0 106.6 %all-reduce.2.cloned.1.call-done = bf16[2,4,500,512]{2,1,3,0:T(4,128)(2,1)} async-done(((bf16[2,4,500,512]{2,1,3,0:T(4,128)(2,1)}), bf16[2,4,500,512]{2,1,3,0:T(4,128)(2,1)}) %all-reduce.2.cloned.1.call-update) | async-done | bytes 4096016 | tf_op jit(solution)/shard_map/psum | solution.py:18
  391.5 5.5 %fusion = bf16[2,4,500,512]{2,1,3,0:T(4,128)(2,1)S(1)} fusion(bf16[2,4,500,512]{2,1,3,0:T(4,128)(2,1)} %all-reduce.2.cloned.1.call-done, f32[4,500,512]{1,0,2:T(4,128)} %broadcast_subtract_fusion), kind=kLoop, calls=%fused_computation.3 | loop fusion | flops 6144000 | bytes 12288000 | tf_op jit(solution)/shard_map/convert_element_type | solution.py:20
  397.1 16.8 %fusion.41 = bf16[2,3000,512]{2,1,0:T(8,128)(2,1)} fusion(bf16[4,3000,500,1]{2,1,0,3:T(8,128)(2,1)} %bitcast.59, bf16[2,4,500,512]{2,1,3,0:T(4,128)(2,1)S(1)} %fusion), kind=kOutput, calls=%fused_computation.6.clone.1 | convolution fusion | flops 12291072000 | bytes 22240000 | tf_op jit(solution)/shard_map/cio,pcov->piv/dot_general | solution.py:21
  413.9 27.6 %convolution_convert_fusion = bf16[2,3000,3000]{2,1,0:T(8,128)(2,1)} fusion(bf16[3000,512]{1,0:T(8,128)(2,1)} %all-gather.4.cloned.1.call-done, bf16[2,3000,512]{2,1,0:T(8,128)(2,1)} %fusion.41), kind=kOutput, calls=%fused_computation | convolution fusion | flops 18449999872 | bytes 45216000 | tf_op jit(solution)/shard_map/piv,jv->pij/dot_general | solution.py:24
Async XLA Ops:
  6.5 33.6 %all-gather.4.cloned.1.call-start = ((), (), s32[]{:S(2)}) async-start(), calls=%async_computation | async-start | bytes 3840000 | tf_op jit(solution)/shard_map/all_gather | solution.py:11
  7.3 247.8 %all-gather.6.cloned.1.call-start = ((), (), s32[]{:S(2)}) async-start(), calls=%async_computation.2 | async-start | bytes 15360000 | tf_op jit(solution)/shard_map/all_gather | solution.py:12
  8.0 383.5 %all-reduce.2.cloned.1.call-start = ((), (), s32[]{:S(2)}) async-start(), calls=%async_computation.1 | async-start | bytes 8388608 | tf_op jit(solution)/shard_map/psum | solution.py:18
  274.2 7.9 %copy-start = (f32[2000]{0:T(1024)S(1)}, f32[2000]{0:T(1024)}, u32[]{:S(2)}) copy-start(f32[2000]{0:T(1024)} %param.8) | copy-start | bytes 24004
  274.2 8.0 %copy-start.1 = (f32[512]{0:T(512)S(1)}, f32[512]{0:T(512)}, u32[]{:S(2)}) copy-start(f32[512]{0:T(512)} %param.9) | copy-start | bytes 6148
Sparse Core Ops, SparseCore 0:
  8.9 31.1 all-gather.3
  41.7 213.3 all-gather.5
  282.2 109.3 all-reduce.1
where the time goes:
time: 448 us
  waiting for transfers between devices  329 us (73%)
  matrix products  89.4 us (20%)
  between operations  13.1 us (3%)
  other arithmetic  8.38 us (2%)
  local copies, waits for them, and re-layouts  7.93 us (2%)
    all_gather x1, waiting for transfers between devices, per_device(): occ_parts = lax.all_gather(occ_coeffs, 'col')  189 us
    psum x1, waiting for transfers between devices, per_device(): coupling = lax.psum(part, ('row', 'col'))  107 us
    all_gather x1, waiting for transfers between devices, per_device(): vir_rows = lax.all_gather(vir_coeffs, 'row', axis=1, tiled=True)  32.1 us
    dot_general x1, matrix products, per_device(): jnp.einsum('piv,jv->pij', mixed, vir_rows, preferred_element_type=F32)  27.6 us
    dot_general x1, matrix products, per_device(): jnp.einsum('pij,jv->piv', perturbation, vir_rows, preferred_element_type=...  25.8 us
    dot_general x1, matrix products, per_device(): jnp.einsum('cio,piv->pcov', occ_parts, image, preferred_element_type=F32)  19.1 us
    dot_general x1, matrix products, per_device(): jnp.einsum('cio,pcov->piv', occ_parts, response, preferred_element_type=F32)  16.8 us
  transfers between devices with their start and end apart: 3, of which 3 were waited for; matrix products, arithmetic and copies ran while one was open for 6% of the time, Pallas kernels for 0%

commit v1 on v0

--- a/solution.py
+++ b/solution.py
@@ -15,7 +15,7 @@
         BF16
     )
     part = jnp.einsum("cio,piv->pcov", occ_parts, image, preferred_element_type=F32).astype(BF16)
-    coupling = lax.psum(part, ("row", "col"))
+    coupling = lax.psum(lax.psum(part, "row"), "col")
     gaps = occ_energies.reshape(cols, width)[:, :, None] - vir_energies[None, None, :]
     response = (coupling.astype(F32) / gaps[None]).astype(BF16)
     mixed = jnp.einsum("cio,pcov->piv", occ_parts, response, preferred_element_type=F32).astype(

time: 448 us -> 580 us (1.29)
  waiting for transfers between devices: 329 us -> 461 us
    psum x1 -> x2, waiting for transfers between devices: 107 us -> 238 us  [per_device(): coupling = lax.psum(lax.psum(part, 'row'), 'col')]
  transfers between devices with their start and end apart: 3 -> 4, of which waited for: 3 -> 4; matrix products, arithmetic and copies ran while one was open for 6% -> 5% of each run, Pallas kernels for 0% -> 0%
where the time goes in v1:
time: 580 us
  waiting for transfers between devices  461 us (79%)
  matrix products  89.4 us (15%)
  between operations  13.1 us (2%)
  other arithmetic  8.39 us (1%)
  local copies, waits for them, and re-layouts  7.9 us (1%)
    psum x2, waiting for transfers between devices, per_device(): coupling = lax.psum(lax.psum(part, 'row'), 'col')  238 us
    all_gather x1, waiting for transfers between devices, per_device(): occ_parts = lax.all_gather(occ_coeffs, 'col')  189 us
    all_gather x1, waiting for transfers between devices, per_device(): vir_rows = lax.all_gather(vir_coeffs, 'row', axis=1, tiled=True)  32.1 us
    dot_general x1, matrix products, per_device(): jnp.einsum('piv,jv->pij', mixed, vir_rows, preferred_element_type=F32)  27.6 us
    dot_general x1, matrix products, per_device(): jnp.einsum('pij,jv->piv', perturbation, vir_rows, preferred_element_type=...  25.8 us
    dot_general x1, matrix products, per_device(): jnp.einsum('cio,piv->pcov', occ_parts, image, preferred_element_type=F32)  19.1 us
    dot_general x1, matrix products, per_device(): jnp.einsum('cio,pcov->piv', occ_parts, response, preferred_element_type=F32)  16.8 us
  transfers between devices with their start and end apart: 4, of which 4 were waited for; matrix products, arithmetic and copies ran while one was open for 5% of the time, Pallas kernels for 0%

profile of v1, /device:TPU:0, one launch (start us, length us, event | category | flops | bytes accessed | tf_op | source)
XLA Modules:
  0.0 579.7 jit_solution(10620880097560044781)
XLA Ops:
  6.5 0.0 all-gather.4.cloned.1.call-start
  6.5 0.7 all-gather.4.cloned.1.call-update
  7.3 0.0 all-gather.6.cloned.1.call-start
  7.3 0.7 all-gather.6.cloned.1.call-update
  8.0 0.0 all-reduce.3.cloned.1.call-start
  8.1 32.1 %all-gather.4.cloned.1.call-done = bf16[3000,512]{1,0:T(8,128)(2,1)} async-done(((bf16[3000,128]{1,0:T(8,128)(2,1)}), bf16[3000,512]{1,0:T(8,128)(2,1)}) %all-gather.4.cloned.1.call-update) | async-done | bytes 3072016 | tf_op jit(solution)/shard_map/all_gather | solution.py:11
  40.1 25.8 %fusion.45 = bf16[2,3000,512,1]{2,1,3,0:T(8,128)(2,1)} fusion(bf16[2,3000,3000]{2,1,0:T(8,128)(2,1)} %param.5, bf16[3000,512]{1,0:T(8,128)(2,1)} %all-gather.4.cloned.1.call-done), kind=kOutput, calls=%fused_computation.5.clone.clone.clone.1 | convolution fusion | flops 18435072000 | bytes 45216000 | tf_op jit(solution)/shard_map/pij,jv->piv/dot_general | solution.py:14
  66.0 189.1 %all-gather.6.cloned.1.call-done = bf16[12000,500]{1,0:T(8,128)(2,1)} async-done(((bf16[3000,500]{1,0:T(8,128)(2,1)}), bf16[12000,500]{1,0:T(8,128)(2,1)}) %all-gather.6.cloned.1.call-update) | async-done | bytes 12000016 | tf_op jit(solution)/shard_map/all_gather | solution.py:12
  255.1 19.1 %fusion.17 = bf16[2,512,4,500]{1,3,2,0:T(8,128)(2,1)} fusion(bf16[4,3000,500,1]{2,1,0,3:T(8,128)(2,1)} %bitcast.58, bf16[2,3000,512,1]{2,1,3,0:T(8,128)(2,1)} %fusion.45), kind=kOutput, calls=%fused_computation.12 | convolution fusion | flops 12290048000 | bytes 22240000 | tf_op jit(solution)/shard_map/cio,piv->pcov/dot_general | solution.py:17
  274.2 7.8 %copy.10 = bf16[2,512,4,500]{3,2,1,0:T(4,128)(2,1)} copy(bf16[2,512,4,500]{1,3,2,0:T(8,128)(2,1)} %fusion.17) | data formatting | bytes 8192000
  282.0 0.0 copy-start
  282.0 0.0 copy-start.1
  282.0 0.0 all-reduce.3.cloned.1.call-update
  282.0 0.2 all-reduce.5.cloned.1.call-start
  282.2 83.6 %all-reduce.3.cloned.1.call-done = bf16[2,4,500,512]{2,1,3,0:T(4,128)(2,1)} async-done(((bf16[2,4,500,512]{2,1,3,0:T(4,128)(2,1)}), bf16[2,4,500,512]{2,1,3,0:T(4,128)(2,1)}) %all-reduce.3.cloned.1.call-update) | async-done | bytes 4096016 | tf_op jit(solution)/shard_map/psum | solution.py:18
  365.8 0.0 all-reduce.5.cloned.1.call-update
  365.8 0.0 copy-done
  365.9 0.1 sub.19
  365.9 0.0 copy-done.1
  365.9 2.8 broadcast_subtract_fusion
  368.8 154.4 %all-reduce.5.cloned.1.call-done = bf16[2,4,500,512]{2,1,3,0:T(4,128)(2,1)} async-done(((bf16[2,4,500,512]{2,1,3,0:T(4,128)(2,1)}), bf16[2,4,500,512]{2,1,3,0:T(4,128)(2,1)}) %all-reduce.5.cloned.1.call-update) | async-done | bytes 4096016 | tf_op jit(solution)/shard_map/psum | solution.py:18
  523.2 5.5 fusion
  528.8 16.8 %fusion.41 = bf16[2,3000,512]{2,1,0:T(8,128)(2,1)} fusion(bf16[4,3000,500,1]{2,1,0,3:T(8,128)(2,1)} %bitcast.59, bf16[2,4,500,512]{2,1,3,0:T(4,128)(2,1)S(1)} %fusion), kind=kOutput, calls=%fused_computation.6.clone.1 | convolution fusion | flops 12291072000 | bytes 22240000 | tf_op jit(solution)/shard_map/cio,pcov->piv/dot_general | solution.py:21
  545.6 27.6 %convolution_convert_fusion = bf16[2,3000,3000]{2,1,0:T(8,128)(2,1)} fusion(bf16[3000,512]{1,0:T(8,128)(2,1)} %all-gather.4.cloned.1.call-done, bf16[2,3000,512]{2,1,0:T(8,128)(2,1)} %fusion.41), kind=kOutput, calls=%fused_computation | convolution fusion | flops 18449999872 | bytes 45216000 | tf_op jit(solution)/shard_map/piv,jv->pij/dot_general | solution.py:24
Async XLA Ops:
  6.5 33.6 %all-gather.4.cloned.1.call-start = ((), (), s32[]{:S(2)}) async-start(), calls=%async_computation | async-start | bytes 3840000 | tf_op jit(solution)/shard_map/all_gather | solution.py:11
  7.3 247.8 %all-gather.6.cloned.1.call-start = ((), (), s32[]{:S(2)}) async-start(), calls=%async_computation.3 | async-start | bytes 15360000 | tf_op jit(solution)/shard_map/all_gather | solution.py:12
  8.0 357.8 %all-reduce.3.cloned.1.call-start = ((), (), s32[]{:S(2)}) async-start(), calls=%async_computation.1 | async-start | bytes 8388608 | tf_op jit(solution)/shard_map/psum | solution.py:18
  282.0 83.9 %copy-start = (f32[2000]{0:T(1024)S(1)}, f32[2000]{0:T(1024)}, u32[]{:S(2)}) copy-start(f32[2000]{0:T(1024)} %param.8) | copy-start | bytes 24004
  282.0 84.0 %copy-start.1 = (f32[512]{0:T(512)S(1)}, f32[512]{0:T(512)}, u32[]{:S(2)}) copy-start(f32[512]{0:T(512)} %param.9) | copy-start | bytes 6148
  282.0 241.2 %all-reduce.5.cloned.1.call-start = ((), (), s32[]{:S(2)}) async-start(), calls=%async_computation.2 | async-start | bytes 8388608 | tf_op jit(solution)/shard_map/psum | solution.py:18
Sparse Core Ops, SparseCore 0:
  8.9 31.1 all-gather.3
  41.7 213.3 all-gather.5
  282.1 83.6 all-reduce.2
  368.0 155.1 all-reduce.4
